TPU v7x, 32 devices: a whole 2x2x4 slice. The times are simulated.
32 devices in a mesh: south: 8 (over z, x), east: 4 (over y, core).
Axes of the slice: x: 2, y: 2, z: 4, core: 2. Of those that a mesh axis runs over, the one named last changes fastest.
Arguments:
- tracer: float32 [256, 128, 128], P('south', 'east'), may hold values from 0.2 to 1.8
- flow_j: float32 [256, 128, 128], P('south', 'east'), may hold values from -0.3 to 0.3
- flow_i: float32 [256, 128, 128], P('south', 'east'), may hold values from -0.3 to 0.3
Outputs:
- running_total: float32 [256, 128, 128], P('south', 'east')
- tracer_end: float32 [256, 128, 128], P('south', 'east')
All inputs are finite; a program needn't handle non-finite values.
Results may differ from a plain program's by a relative error of at most 0.00002.
Values sent between devices are 32-bit elements; how exact they have to be, the bound alone decides.
A program may use at most 64 MiB of HBM per device.

v0:
```python
import jax
import jax.numpy as jnp
from jax import lax
from jax.sharding import PartitionSpec as P

STEPS = 4


def extended(cells, sides, width):
    for axis, dim in sides:
        count = lax.axis_size(axis)
        ends = count - 1
        head = lax.slice_in_dim(cells, 0, width, axis=dim)
        tail = lax.slice_in_dim(cells, cells.shape[dim] - width, cells.shape[dim], axis=dim)
        cells = jnp.concatenate(
            [
                lax.ppermute(tail, axis, [(i, (i + 1) % count) for i in range(ends)]),
                cells,
                lax.ppermute(head, axis, [((i + 1) % count, i) for i in range(ends)]),
            ],
            axis=dim,
        )
    return cells


def carried_in(part, axis, combine, identity):
    place = lax.axis_index(axis)
    gathered = lax.all_gather(part, axis)
    state = jnp.zeros_like(part) + jnp.asarray(identity, part.dtype)

    def one(turn, state):
        return combine(state, lax.dynamic_index_in_dim(gathered, turn, 0, False))

    return lax.fori_loop(0, place, one, state)


def inner_cells(values, dims):
    for dim in dims:
        values = lax.slice_in_dim(values, 1, values.shape[dim] - 1, axis=dim)
    return values


def side_cells(values, dim, start, dims):
    others = [other for other in dims if other != dim]
    values = inner_cells(values, others)
    return lax.slice_in_dim(values, start, start + values.shape[dim] - 2, axis=dim)


def advance(padded, flow_j, flow_i):
    middle = inner_cells(padded, (0, 1))
    lower = [side_cells(padded, dim, 0, (0, 1)) for dim in (0, 1)]
    upper = [side_cells(padded, dim, 2, (0, 1)) for dim in (0, 1)]
    slopes = [above - below for above, below in zip(upper, lower)]
    smooth_rate = 0.05
    spread = lower[0] + upper[0] + lower[1] + upper[1] - 4.0 * middle
    return middle - flow_j * slopes[0] - flow_i * slopes[1] + smooth_rate * spread


def per_device(tracer, flow_j, flow_i):
    padded = extended(tracer, (("south", 0), ("east", 1)), STEPS)
    wide_parts = extended(
        jnp.concatenate([flow_j, flow_i], axis=2), (("south", 0), ("east", 1)), STEPS - 1
    )
    wide_flow_j, wide_flow_i = jnp.split(wide_parts, 2, axis=2)
    for step in range(STEPS):
        later = advance(padded, wide_flow_j, wide_flow_i)
        values = later
        margin = STEPS - 1 - step
        place = lax.axis_index("south") * tracer.shape[0] - margin + jnp.arange(values.shape[0])
        keep_cells = (place >= 0) & (place < tracer.shape[0] * lax.axis_size("south"))
        values = jnp.where(keep_cells.reshape((-1,) + (1,) * 2), values, 0.0)
        place = lax.axis_index("east") * tracer.shape[1] - margin + jnp.arange(values.shape[1])
        keep_cells = (place >= 0) & (place < tracer.shape[1] * lax.axis_size("east"))
        values = jnp.where(keep_cells.reshape((-1,) + (1,) * 1), values, 0.0)
        later = values
        if step < STEPS - 1:
            wide_flow_j = inner_cells(wide_flow_j, (0, 1))
            wide_flow_i = inner_cells(wide_flow_i, (0, 1))
        padded = later
    tracer = padded
    here = jnp.cumsum(tracer, axis=0)
    total = lax.slice_in_dim(here, here.shape[0] - 1, here.shape[0], axis=0)

    def add_pair(earlier_total, later_total):
        return earlier_total + later_total

    below = carried_in(total, "south", add_pair, jnp.zeros_like(total))
    running_total = (here + below) / (tracer.shape[0] * lax.axis_size("south"))
    return (running_total, tracer)


def solution(mesh):
    in_specs = (P("south", "east", None), P("south", "east", None), P("south", "east", None))
    out_specs = (P("south", "east", None), P("south", "east", None))
    return jax.shard_map(
        per_device, mesh=mesh, in_specs=in_specs, out_specs=out_specs, check_vma=False
    )
```

profile of v0, /device:TPU:4, one launch (start us, length us, event | category | flops | bytes accessed | tf_op | source)
XLA Modules:
  0.0 69.2 jit_solution(3142327858014248375)
XLA Ops:
  0.6 1.1 %constant_dynamic-update-slice_fusion.4 = f32[32,32,256]{2,1,0:T(8,128)S(1)} fusion(f32[32,32,128]{2,1,0:T(8,128)} %param.6), kind=kLoop, calls=%fused_computation.33 | loop fusion | bytes 1048576
  1.8 1.1 %constant_dynamic-update-slice_fusion.3 = f32[32,32,256]{2,1,0:T(8,128)S(1)} fusion(f32[32,32,256]{2,1,0:T(8,128)S(1)} %constant_dynamic-update-slice_fusion.4, f32[32,32,128]{2,1,0:T(8,128)} %param.7), kind=kLoop, calls=%fused_computation.32 | loop fusion | bytes 1048576 | tf_op jit(solution)/shard_map/concatenate | solution.py:62
  2.9 3.4 %collective-permute-start.4 = (f32[3,32,256]{2,1,0:T(8,128)S(1)}, f32[3,32,256]{2,1,0:T(8,128)S(1)}, u32[]{:S(2)}, u32[]{:S(2)}) collective-permute-start(f32[3,32,256]{2,1,0:T(8,128)S(1)} %get-tuple-element.44), channel_id=1, source_target_pairs={{0,4},{4,8},{8,12},{12,16},{16,20},{20,24},{24,28},{1,5},{5,9},{9,... | collective-permute-start | bytes 294920 | tf_op jit(solution)/shard_map/ppermute | solution.py:17
  6.3 1.3 %collective-permute-start.5 = (f32[3,32,256]{2,1,0:T(8,128)S(1)}, f32[3,32,256]{2,1,0:T(8,128)S(1)}, u32[]{:S(2)}, u32[]{:S(2)}) collective-permute-start(f32[3,32,256]{2,1,0:T(8,128)S(1)} %get-tuple-element.45), channel_id=1, source_target_pairs={{4,0},{8,4},{12,8},{16,12},{20,16},{24,20},{28,24},{5,1},{9,5},{13... | collective-permute-start | bytes 294920 | tf_op jit(solution)/shard_map/ppermute | solution.py:19
  7.6 4.5 %collective-permute-start = (f32[4,32,128]{2,1,0:T(8,128)S(1)}, f32[4,32,128]{2,1,0:T(8,128)S(1)}, u32[]{:S(2)}, u32[]{:S(2)}) collective-permute-start(f32[4,32,128]{2,1,0:T(8,128)S(1)} %get-tuple-element.49), channel_id=1, source_target_pairs={{0,4},{4,8},{8,12},{12,16},{16,20},{20,24},{24,28},{1,5},{5,9},{9,... | collective-permute-start | bytes 196616 | tf_op jit(solution)/shard_map/ppermute | solution.py:17
  12.2 1.3 %collective-permute-start.1 = (f32[4,32,128]{2,1,0:T(8,128)S(1)}, f32[4,32,128]{2,1,0:T(8,128)S(1)}, u32[]{:S(2)}, u32[]{:S(2)}) collective-permute-start(f32[4,32,128]{2,1,0:T(8,128)S(1)} %get-tuple-element.48), channel_id=1, source_target_pairs={{4,0},{8,4},{12,8},{16,12},{20,16},{24,20},{28,24},{5,1},{9,5},{13... | collective-permute-start | bytes 196616 | tf_op jit(solution)/shard_map/ppermute | solution.py:19
  13.6 0.5 collective-permute-done
  14.1 4.7 %collective-permute-done.1 = f32[4,32,128]{2,1,0:T(8,128)S(1)} collective-permute-done((f32[4,32,128]{2,1,0:T(8,128)S(1)}, f32[4,32,128]{2,1,0:T(8,128)S(1)}, u32[]{:S(2)}, u32[]{:S(2)}) %collective-permute-start.1) | collective-permute-done | bytes 65568 | tf_op jit(solution)/shard_map/ppermute | solution.py:19
  18.8 1.9 %collective-permute-start.2 = (f32[40,4,128]{2,1,0:T(4,128)S(1)}, f32[40,4,128]{2,1,0:T(4,128)S(1)}, u32[]{:S(2)}, u32[]{:S(2)}) collective-permute-start(f32[40,4,128]{2,1,0:T(4,128)S(1)} %get-tuple-element.46), channel_id=1, source_target_pairs={{0,1},{1,2},{2,3},{4,5},{5,6},{6,7},{8,9},{9,10},{10,11},{12,13},{... | collective-permute-start | bytes 245768 | tf_op jit(solution)/shard_map/ppermute | solution.py:17
  20.7 3.6 %collective-permute-start.3 = (f32[40,4,128]{2,1,0:T(4,128)S(1)}, f32[40,4,128]{2,1,0:T(4,128)S(1)}, u32[]{:S(2)}, u32[]{:S(2)}) collective-permute-start(f32[40,4,128]{2,1,0:T(4,128)S(1)} %get-tuple-element.47), channel_id=1, source_target_pairs={{1,0},{2,1},{3,2},{5,4},{6,5},{7,6},{9,8},{10,9},{11,10},{13,12},{... | collective-permute-start | bytes 245768 | tf_op jit(solution)/shard_map/ppermute | solution.py:19
  24.4 0.0 collective-permute-done.4
  24.4 0.0 collective-permute-done.5
  24.4 0.1 pad_maximum_fusion.4
  24.5 1.9 %collective-permute-start.6 = (f32[38,3,256]{2,1,0:T(4,128)S(1)}, f32[38,3,256]{2,1,0:T(4,128)S(1)}, u32[]{:S(2)}, u32[]{:S(2)}) collective-permute-start(f32[38,3,256]{2,1,0:T(4,128)S(1)} %get-tuple-element.42), channel_id=1, source_target_pairs={{0,1},{1,2},{2,3},{4,5},{5,6},{6,7},{8,9},{9,10},{10,11},{12,13},{... | collective-permute-start | bytes 350216 | tf_op jit(solution)/shard_map/ppermute | solution.py:17
  26.4 3.6 %collective-permute-start.7 = (f32[38,3,256]{2,1,0:T(4,128)S(1)}, f32[38,3,256]{2,1,0:T(4,128)S(1)}, u32[]{:S(2)}, u32[]{:S(2)}) collective-permute-start(f32[38,3,256]{2,1,0:T(4,128)S(1)} %get-tuple-element.43), channel_id=1, source_target_pairs={{1,0},{2,1},{3,2},{5,4},{6,5},{7,6},{9,8},{10,9},{11,10},{13,12},{... | collective-permute-start | bytes 350216 | tf_op jit(solution)/shard_map/ppermute | solution.py:19
  30.1 0.0 collective-permute-done.2
  30.1 0.1 pad_maximum_fusion.1
  30.2 0.8 %collective-permute-done.6 = f32[38,3,256]{2,1,0:T(4,128)S(1)} collective-permute-done((f32[38,3,256]{2,1,0:T(4,128)S(1)}, f32[38,3,256]{2,1,0:T(4,128)S(1)}, u32[]{:S(2)}, u32[]{:S(2)}) %collective-permute-start.6) | collective-permute-done | bytes 116768 | tf_op jit(solution)/shard_map/ppermute | solution.py:17
  31.0 1.8 %collective-permute-done.7 = f32[38,3,256]{2,1,0:T(4,128)S(1)} collective-permute-done((f32[38,3,256]{2,1,0:T(4,128)S(1)}, f32[38,3,256]{2,1,0:T(4,128)S(1)}, u32[]{:S(2)}, u32[]{:S(2)}) %collective-permute-start.7) | collective-permute-done | bytes 116768 | tf_op jit(solution)/shard_map/ppermute | solution.py:19
  32.8 0.2 pad_maximum_fusion
  33.0 0.5 fusion.3
  33.6 0.6 fusion.8
  34.2 0.0 copy-start
  34.2 0.0 copy-start.1
  34.2 0.6 fusion.13
  34.8 0.4 copy-done
  35.2 0.2 copy-done.1
  35.4 0.4 select_select_fusion
  35.7 0.0 copy-start.2
  35.8 2.0 %fusion.18 = f32[32,32,128]{2,1,0:T(8,128)S(1)} fusion(f32[32,32,128]{2,1,0:T(8,128)S(1)} %select_select_fusion), kind=kOutput, calls=%fused_computation.45 | output fusion | flops 4063232 | bytes 1048576 | tf_op jit(solution)/shard_map/jit(cumsum)/reduce_window_sum | solution.py:81
  37.8 30.5 %all-gather = f32[8,32,128]{2,1,0:T(8,128)S(1)} all-gather(f32[1,32,128]{2,1,0:T(8,128)S(1)} %slice.224), channel_id=2, replica_groups=mesh['south'=8,'east'=4] {'south'}, dimensions={0}, use_global_device_ids=true | all-gather | bytes 147456 | tf_op jit(solution)/shard_map/all_gather | solution.py:28
  68.3 0.9 %add_multiply_fusion = f32[32,32,128]{2,1,0:T(8,128)} fusion(f32[32,32,128]{2,1,0:T(8,128)S(1)} %fusion.18, f32[32,128]{1,0:T(8,128)S(1)} %bitcast.9), kind=kLoop, calls=%fused_computation.24 | loop fusion | flops 262144 | bytes 1064960 | tf_op jit(solution)/shard_map/div | solution.py:88
  (17 shorter events, 0.2 us)
Async XLA Ops:
  0.6 7.0 %copy-start.3 = (f32[32,32,128]{2,1,0:T(8,128)S(1)}, f32[32,32,128]{2,1,0:T(8,128)}, u32[]{:S(2)}) copy-start(f32[32,32,128]{2,1,0:T(8,128)} %param.5) | copy-start | bytes 1572868
  2.9 21.5 %collective-permute-start.4 = (f32[3,32,256]{2,1,0:T(8,128)S(1)}, f32[3,32,256]{2,1,0:T(8,128)S(1)}, u32[]{:S(2)}, u32[]{:S(2)}) collective-permute-start(f32[3,32,256]{2,1,0:T(8,128)S(1)} %get-tuple-element.44), channel_id=1, source_target_pairs={{0,4},{4,8},{8,12},{12,16},{16,20},{20,24},{24,28},{1,5},{5,9},{9,... | collective-permute-start | bytes 294920 | tf_op jit(solution)/shard_map/ppermute | solution.py:17
  6.3 18.1 %collective-permute-start.5 = (f32[3,32,256]{2,1,0:T(8,128)S(1)}, f32[3,32,256]{2,1,0:T(8,128)S(1)}, u32[]{:S(2)}, u32[]{:S(2)}) collective-permute-start(f32[3,32,256]{2,1,0:T(8,128)S(1)} %get-tuple-element.45), channel_id=1, source_target_pairs={{4,0},{8,4},{12,8},{16,12},{20,16},{24,20},{28,24},{5,1},{9,5},{13... | collective-permute-start | bytes 294920 | tf_op jit(solution)/shard_map/ppermute | solution.py:19
  7.6 6.4 %collective-permute-start = (f32[4,32,128]{2,1,0:T(8,128)S(1)}, f32[4,32,128]{2,1,0:T(8,128)S(1)}, u32[]{:S(2)}, u32[]{:S(2)}) collective-permute-start(f32[4,32,128]{2,1,0:T(8,128)S(1)} %get-tuple-element.49), channel_id=1, source_target_pairs={{0,4},{4,8},{8,12},{12,16},{16,20},{20,24},{24,28},{1,5},{5,9},{9,... | collective-permute-start | bytes 196616 | tf_op jit(solution)/shard_map/ppermute | solution.py:17
  12.2 6.6 %collective-permute-start.1 = (f32[4,32,128]{2,1,0:T(8,128)S(1)}, f32[4,32,128]{2,1,0:T(8,128)S(1)}, u32[]{:S(2)}, u32[]{:S(2)}) collective-permute-start(f32[4,32,128]{2,1,0:T(8,128)S(1)} %get-tuple-element.48), channel_id=1, source_target_pairs={{4,0},{8,4},{12,8},{16,12},{20,16},{24,20},{28,24},{5,1},{9,5},{13... | collective-permute-start | bytes 196616 | tf_op jit(solution)/shard_map/ppermute | solution.py:19
  18.8 11.2 %collective-permute-start.2 = (f32[40,4,128]{2,1,0:T(4,128)S(1)}, f32[40,4,128]{2,1,0:T(4,128)S(1)}, u32[]{:S(2)}, u32[]{:S(2)}) collective-permute-start(f32[40,4,128]{2,1,0:T(4,128)S(1)} %get-tuple-element.46), channel_id=1, source_target_pairs={{0,1},{1,2},{2,3},{4,5},{5,6},{6,7},{8,9},{9,10},{10,11},{12,13},{... | collective-permute-start | bytes 245768 | tf_op jit(solution)/shard_map/ppermute | solution.py:17
  20.7 9.3 %collective-permute-start.3 = (f32[40,4,128]{2,1,0:T(4,128)S(1)}, f32[40,4,128]{2,1,0:T(4,128)S(1)}, u32[]{:S(2)}, u32[]{:S(2)}) collective-permute-start(f32[40,4,128]{2,1,0:T(4,128)S(1)} %get-tuple-element.47), channel_id=1, source_target_pairs={{1,0},{2,1},{3,2},{5,4},{6,5},{7,6},{9,8},{10,9},{11,10},{13,12},{... | collective-permute-start | bytes 245768 | tf_op jit(solution)/shard_map/ppermute | solution.py:19
  24.5 6.5 %collective-permute-start.6 = (f32[38,3,256]{2,1,0:T(4,128)S(1)}, f32[38,3,256]{2,1,0:T(4,128)S(1)}, u32[]{:S(2)}, u32[]{:S(2)}) collective-permute-start(f32[38,3,256]{2,1,0:T(4,128)S(1)} %get-tuple-element.42), channel_id=1, source_target_pairs={{0,1},{1,2},{2,3},{4,5},{5,6},{6,7},{8,9},{9,10},{10,11},{12,13},{... | collective-permute-start | bytes 350216 | tf_op jit(solution)/shard_map/ppermute | solution.py:17
  26.4 6.4 %collective-permute-start.7 = (f32[38,3,256]{2,1,0:T(4,128)S(1)}, f32[38,3,256]{2,1,0:T(4,128)S(1)}, u32[]{:S(2)}, u32[]{:S(2)}) collective-permute-start(f32[38,3,256]{2,1,0:T(4,128)S(1)} %get-tuple-element.43), channel_id=1, source_target_pairs={{1,0},{2,1},{3,2},{5,4},{6,5},{7,6},{9,8},{10,9},{11,10},{13,12},{... | collective-permute-start | bytes 350216 | tf_op jit(solution)/shard_map/ppermute | solution.py:19
  34.2 1.0 %copy-start = (f32[32,32,128]{2,1,0:T(8,128)S(1)}, f32[32,32,128]{2,1,0:T(8,128)}, u32[]{:S(2)}) copy-start(f32[32,32,128]{2,1,0:T(8,128)} %param.7) | copy-start | bytes 1572868
  34.2 1.2 %copy-start.1 = (f32[32,32,128]{2,1,0:T(8,128)S(1)}, f32[32,32,128]{2,1,0:T(8,128)}, u32[]{:S(2)}) copy-start(f32[32,32,128]{2,1,0:T(8,128)} %param.6) | copy-start | bytes 1572868
  35.7 33.4 %copy-start.2 = (f32[32,32,128]{2,1,0:T(8,128)}, f32[32,32,128]{2,1,0:T(8,128)S(1)}, u32[]{:S(2)}) copy-start(f32[32,32,128]{2,1,0:T(8,128)S(1)} %select_select_fusion) | copy-start | bytes 1572868
where the time goes:
time: 69.5 us; the launch traced here: 69.2 us
  blocking collectives  30.5 us (44%)
  starting transfers between devices  21.7 us (31%)
  waiting for transfers between devices  7.78 us (11%)
  other arithmetic  5.38 us (8%)
  local copies, waits for them, and re-layouts  2.93 us (4%)
  between operations  0.89 us (1%)
    all_gather x1, blocking collectives, carried_in(): gathered = lax.all_gather(part, axis)  30.5 us
    ppermute x4, starting transfers between devices, extended(): lax.ppermute(tail, axis, [(i, (i + 1) % count) for i in range(ends)])  11.8 us
    ppermute x4, starting transfers between devices, extended(): lax.ppermute(head, axis, [((i + 1) % count, i) for i in range(ends)])  9.87 us
    ppermute x4, waiting for transfers between devices, extended(): lax.ppermute(head, axis, [((i + 1) % count, i) for i in range(ends)])  6.43 us
    select_n x4, other arithmetic, per_device(): values = jnp.where(keep_cells.reshape((-1,) + (1,) * 1), values, 0.0)  2.11 us
    another operation x1, other arithmetic, per_device(): here = jnp.cumsum(tracer, axis=0)  2 us
    unnamed x11, local copies, waits for them, and re-layouts  1.78 us
  transfers between devices with their start and end apart: 8, of which 4 were waited for; matrix products, arithmetic and copies ran while one was open for 0% of the time, Pallas kernels for 0%

commit v1 on v0

v1 whole, which is shorter than its diff:
```python
import functools

import jax
import jax.numpy as jnp
from jax import lax
from jax.experimental import pallas as pl
from jax.experimental.pallas import tpu as pltpu
from jax.sharding import PartitionSpec as P

STEPS = 4
TILE = 8


def chunk_of(rows, most):
    return max(c for c in range(1, most + 1) if rows % c == 0)


def advance(level, flow_j, flow_i, row, rows, col, cols):
    def at(dj, di):
        return level[pl.ds(row + 1 + dj, rows), pl.ds(col + TILE + di, cols), :]

    middle, lower_j, upper_j, lower_i, upper_i = at(0, 0), at(-1, 0), at(1, 0), at(0, -1), at(0, 1)
    fj = flow_j[pl.ds(row, rows), pl.ds(col, cols), :]
    fi = flow_i[pl.ds(row, rows), pl.ds(col, cols), :]
    spread = lower_j + upper_j + lower_i + upper_i - 4.0 * middle
    return middle - fj * (upper_j - lower_j) - fi * (upper_i - lower_i) + 0.05 * spread


def kernel(souths, easts, tracer, flow_j, flow_i, running, end, level0, level1, level2, level3, fj, fi, own, totals,
           load_sem, send_sem, recv_sem, total_send, total_recv):
    J, I, _ = tracer.shape
    s, e = lax.axis_index("south"), lax.axis_index("east")
    levels = (level0, level1, level2, level3)
    loads = [
        pltpu.make_async_copy(tracer, level0.at[pl.ds(1, J), pl.ds(TILE, I), :], load_sem.at[0]),
        pltpu.make_async_copy(flow_j, fj, load_sem.at[1]),
        pltpu.make_async_copy(flow_i, fi, load_sem.at[2]),
    ]
    for load in loads:
        load.start()

    sides = (
        (s > 0, {"south": s - 1, "east": e}),
        (s < souths - 1, {"south": s + 1, "east": e}),
        (e > 0, {"south": s, "east": e - 1}),
        (e < easts - 1, {"south": s, "east": e + 1}),
    )
    barrier = pltpu.get_barrier_semaphore()
    for exists, peer in sides[2:]:
        @pl.when(exists)
        def _(peer=peer):
            pl.semaphore_signal(barrier, inc=1, device_id=peer, device_id_type=pl.DeviceIdType.MESH)

    def greet(turn, _):
        other = lax.rem(s + turn, souths)
        pl.semaphore_signal(barrier, inc=1, device_id={"south": other, "east": e},
                            device_id_type=pl.DeviceIdType.MESH)
        return 0

    lax.fori_loop(1, souths, greet, 0)

    row_zero = jnp.zeros((1, I, tracer.shape[2]), jnp.float32)
    col_zero = jnp.zeros((J, TILE, tracer.shape[2]), jnp.float32)
    for level in levels:
        @pl.when(s == 0)
        def _(level=level):
            level[0:1, TILE:TILE + I, :] = row_zero

        @pl.when(s == souths - 1)
        def _(level=level):
            level[J + 1:J + 2, TILE:TILE + I, :] = row_zero

        @pl.when(e == 0)
        def _(level=level):
            level[1:J + 1, 0:TILE, :] = col_zero

        @pl.when(e == easts - 1)
        def _(level=level):
            level[1:J + 1, TILE + I:2 * TILE + I, :] = col_zero

    near = (e > 0).astype(jnp.int32) + (e < easts - 1).astype(jnp.int32)
    pl.semaphore_wait(barrier, souths - 1 + near)

    def copies(k):
        level = levels[k]
        own_cols, own_rows = pl.ds(TILE, I), pl.ds(1, J)
        moves = (
            ((pl.ds(1, 1), own_cols), (pl.ds(J + 1, 1), own_cols)),
            ((pl.ds(J, 1), own_cols), (pl.ds(0, 1), own_cols)),
            ((own_rows, pl.ds(TILE, TILE)), (own_rows, pl.ds(TILE + I, TILE))),
            ((own_rows, pl.ds(I, TILE)), (own_rows, pl.ds(0, TILE))),
        )
        out = []
        for side, ((exists, peer), (src, dst)) in enumerate(zip(sides, moves)):
            copy = pltpu.make_async_remote_copy(
                src_ref=level.at[src[0], src[1], :], dst_ref=level.at[dst[0], dst[1], :],
                send_sem=send_sem.at[k, side], recv_sem=recv_sem.at[k, side],
                device_id=peer, device_id_type=pl.DeviceIdType.MESH)
            out.append((exists, copy))
        return out

    def start(k, which):
        for side in which:
            exists, copy = copies(k)[side]
            pl.when(exists)(copy.start)

    def receive(k):
        for side, opposite in enumerate((1, 0, 3, 2)):
            exists = sides[side][0]
            copy = copies(k)[opposite][1]
            pl.when(exists)(copy.wait_recv)

    def put(k, row, rows, col, cols, value):
        if k == STEPS:
            end[pl.ds(row, rows), pl.ds(col, cols), :] = value
        else:
            levels[k][pl.ds(row + 1, rows), pl.ds(col + TILE, cols), :] = value

    def sweep(k, col, cols):
        rows = chunk_of(J - 2, 6)

        def body(turn, _):
            row = 1 + turn * rows
            put(k, row, rows, col, cols, advance(levels[k - 1], fj, fi, row, rows, col, cols))
            return 0

        lax.fori_loop(0, (J - 2) // rows, body, 0)

    def edge_rows(k):
        for row in (0, J - 1):
            put(k, row, 1, 0, I, advance(levels[k - 1], fj, fi, row, 1, 0, I))

    loads[0].wait()
    start(0, range(4))
    loads[1].wait()
    loads[2].wait()
    for k in range(1, STEPS + 1):
        sweep(k, TILE, I - 2 * TILE)
        receive(k - 1)
        edge_rows(k)
        if k < STEPS:
            start(k, (0, 1))
        sweep(k, 0, TILE)
        sweep(k, I - TILE, TILE)
        if k < STEPS:
            start(k, (2, 3))

    total = end[0]
    for row in range(1, J):
        total = total + end[row]
    own[...] = total

    def total_copy(source, other):
        return pltpu.make_async_remote_copy(
            src_ref=own, dst_ref=totals.at[source], send_sem=total_send.at[other], recv_sem=total_recv.at[source],
            device_id={"south": other, "east": e}, device_id_type=pl.DeviceIdType.MESH)

    def give(turn, _):
        total_copy(s, s + turn).start()
        return 0

    lax.fori_loop(1, souths - s, give, 0)

    for k in range(STEPS):
        for exists, copy in copies(k):
            pl.when(exists)(copy.wait_send)

    def take(source, state):
        total_copy(source, s).wait_recv()
        return state + totals[source]

    state = lax.fori_loop(0, s, take, jnp.zeros_like(own))
    scale = 1.0 / (J * souths)
    for row in range(J):
        state = state + end[row]
        running[row] = state * scale

    def sent(turn, _):
        total_copy(s, s + turn).wait_send()
        return 0

    lax.fori_loop(1, souths - s, sent, 0)


def per_device(souths, easts, tracer, flow_j, flow_i):
    J, I, M = tracer.shape
    out = jax.ShapeDtypeStruct((J, I, M), jnp.float32)
    return pl.pallas_call(
        functools.partial(kernel, souths, easts),
        out_shape=(out, out),
        in_specs=[pl.BlockSpec(memory_space=pl.ANY)] * 3,
        out_specs=(pl.BlockSpec(memory_space=pltpu.VMEM),) * 2,
        scratch_shapes=[pltpu.VMEM((J + 2, I + 2 * TILE, M), jnp.float32)] * STEPS
        + [pltpu.VMEM((J, I, M), jnp.float32)] * 2
        + [
            pltpu.VMEM((I, M), jnp.float32),
            pltpu.VMEM((souths, I, M), jnp.float32),
            pltpu.SemaphoreType.DMA((3,)),
            pltpu.SemaphoreType.DMA((STEPS, 4)),
            pltpu.SemaphoreType.DMA((STEPS, 4)),
            pltpu.SemaphoreType.DMA((souths,)),
            pltpu.SemaphoreType.DMA((souths,)),
        ],
        compiler_params=pltpu.CompilerParams(collective_id=0, has_side_effects=True,
                                             vmem_limit_bytes=24 * 2 ** 20),
    )(tracer, flow_j, flow_i)


def solution(mesh):
    spec = P("south", "east", None)
    body = functools.partial(per_device, mesh.shape["south"], mesh.shape["east"])
    return jax.shard_map(body, mesh=mesh, in_specs=(spec,) * 3, out_specs=(spec,) * 2, check_vma=False)
```

time: 69.5 us -> 28.8 us (0.41)
  the two profiles are of different devices: /device:TPU:4 before, /device:TPU:30 now
where the time goes in v1:
time: 28.8 us; the launch traced here: 28.6 us
  Pallas kernels  23.2 us (81%)
  local copies, waits for them, and re-layouts  4.71 us (16%)
  between operations  0.65 us (2%)
    pallas_call x1, Pallas kernels, per_device(): pl.pallas_call(functools.partial(kernel, souths, easts), out_shape=(out,...  23.2 us
    unnamed x8, local copies, waits for them, and re-layouts  4.71 us

profile of v1, /device:TPU:30, one launch (start us, length us, event | category | flops | bytes accessed | tf_op | source)
XLA Modules:
  0.0 28.6 jit_solution(1280042414063021634)
XLA Ops:
  0.6 0.0 copy-start
  0.6 1.0 %copy-done = f32[32,32,128]{2,1,0:T(8,128)S(1)} copy-done((f32[32,32,128]{2,1,0:T(8,128)S(1)}, f32[32,32,128]{2,1,0:T(8,128)}, u32[]{:S(2)}) %copy-start) | copy-done | bytes 524312
  1.7 0.0 copy-start.1
  1.7 1.0 %copy-done.1 = f32[32,32,128]{2,1,0:T(8,128)S(1)} copy-done((f32[32,32,128]{2,1,0:T(8,128)S(1)}, f32[32,32,128]{2,1,0:T(8,128)}, u32[]{:S(2)}) %copy-start.1) | copy-done | bytes 524312
  2.7 0.0 copy-start.2
  2.7 1.0 %copy-done.2 = f32[32,32,128]{2,1,0:T(8,128)S(1)} copy-done((f32[32,32,128]{2,1,0:T(8,128)S(1)}, f32[32,32,128]{2,1,0:T(8,128)}, u32[]{:S(2)}) %copy-start.2) | copy-done | bytes 524312
  3.8 23.2 %shard_map.50 = (f32[32,32,128]{2,1,0:T(8,128)S(1)}, f32[32,32,128]{2,1,0:T(8,128)S(1)}) custom-call(f32[32,32,128]{2,1,0:T(8,128)S(1)} %copy-done, f32[32,32,128]{2,1,0:T(8,128)S(1)} %copy-done.1, f32[32,32,128]{2,1,0:T(8,128)S(1)} %copy-done.2), custom_call_target="tpu_custom_call" | custom-call | tf_op jit(solution)/shard_map/pallas_call | solution.py:188
  27.0 0.8 %copy.7 = f32[32,32,128]{2,1,0:T(8,128)} copy(f32[32,32,128]{2,1,0:T(8,128)S(1)} %get-tuple-element.4) | data formatting | bytes 1048576
  27.8 0.8 %copy.8 = f32[32,32,128]{2,1,0:T(8,128)} copy(f32[32,32,128]{2,1,0:T(8,128)S(1)} %get-tuple-element.5) | data formatting | bytes 1048576
Async XLA Ops:
  0.6 1.0 %copy-start = (f32[32,32,128]{2,1,0:T(8,128)S(1)}, f32[32,32,128]{2,1,0:T(8,128)}, u32[]{:S(2)}) copy-start(f32[32,32,128]{2,1,0:T(8,128)} %tracer.1) | copy-start | bytes 1572868
  1.7 1.0 %copy-start.1 = (f32[32,32,128]{2,1,0:T(8,128)S(1)}, f32[32,32,128]{2,1,0:T(8,128)}, u32[]{:S(2)}) copy-start(f32[32,32,128]{2,1,0:T(8,128)} %flow_j.1) | copy-start | bytes 1572868
  2.7 1.0 %copy-start.2 = (f32[32,32,128]{2,1,0:T(8,128)S(1)}, f32[32,32,128]{2,1,0:T(8,128)}, u32[]{:S(2)}) copy-start(f32[32,32,128]{2,1,0:T(8,128)} %flow_i.1) | copy-start | bytes 1572868

commit v2 on v1

v2 whole, which is shorter than its diff:
```python
import functools

import jax
import jax.numpy as jnp
from jax import lax
from jax.experimental import pallas as pl
from jax.experimental.pallas import tpu as pltpu
from jax.sharding import PartitionSpec as P

ROUNDS = (1, 3)
STEPS = sum(ROUNDS)
DEEP = max(ROUNDS)
TILE = 8
MESH = pl.DeviceIdType.MESH
SIDES = ((-1, 0), (1, 0), (-1, -1), (-1, 1), (1, -1), (1, 1), (0, -1), (0, 1))


def plan():
    out, base = [], 0
    for turn, depth in enumerate(ROUNDS):
        out += [(base, side, depth) for side in SIDES]
        if turn == 0:
            out += [(name, side, DEEP - 1) for name in ("fj", "fi") for side in SIDES]
        base += depth
    return [(a, side, d - 1 if all(side) else d) for a, side, d in out if d - (1 if all(side) else 0) > 0]


MESSAGES = plan()


def chunk_of(rows, most):
    return max(c for c in range(1, most + 1) if rows % c == 0)


def view(ref, row, rows, col, cols):
    return ref.at[pl.ds(row + DEEP, rows), pl.ds(col + TILE, cols), :]


def advance(level, flow_j, flow_i, *area):
    row, rows, col, cols = area

    def at(dj, di):
        return view(level, row + dj, rows, col + di, cols)[...]

    middle, lower_j, upper_j, lower_i, upper_i = at(0, 0), at(-1, 0), at(1, 0), at(0, -1), at(0, 1)
    spread = lower_j + upper_j + lower_i + upper_i - 4.0 * middle
    return (middle - view(flow_j, *area)[...] * (upper_j - lower_j)
            - view(flow_i, *area)[...] * (upper_i - lower_i) + 0.05 * spread)


def kernel(souths, easts, tracer, flow_j, flow_i, running, end, level0, level1, level2, level3, fj, fi, own, totals,
           load_sem, send_sem, recv_sem, total_send, total_recv):
    J, I, M = tracer.shape
    s, e = lax.axis_index("south"), lax.axis_index("east")
    levels = (level0, level1, level2, level3)
    arrays = {0: level0, 1: level1, 2: level2, 3: level3, "fj": fj, "fi": fi}
    loads = [pltpu.make_async_copy(src, view(dst, 0, J, 0, I), load_sem.at[k])
             for k, (src, dst) in enumerate(((tracer, level0), (flow_j, fj), (flow_i, fi)))]
    for load in loads:
        load.start()

    def exists(side):
        tests = [test for step, test in ((side[0] + 5, s > 0), (side[0] + 3, s < souths - 1),
                                         (side[1] + 5, e > 0), (side[1] + 3, e < easts - 1)) if step == 4]
        return functools.reduce(jnp.logical_and, tests)

    def peer(side):
        return {"south": s + side[0], "east": e + side[1]}

    barrier = pltpu.get_barrier_semaphore()
    near = souths - 1
    for side in SIDES:
        if side[1] and (DEEP > 1 or not side[0]):
            near = near + exists(side).astype(jnp.int32)

            @pl.when(exists(side))
            def _(side=side):
                pl.semaphore_signal(barrier, inc=1, device_id=peer(side), device_id_type=MESH)

    def greet(turn, _):
        other = lax.rem(s + turn, souths)
        pl.semaphore_signal(barrier, inc=1, device_id={"south": other, "east": e}, device_id_type=MESH)
        return 0

    lax.fori_loop(1, souths, greet, 0)

    def clear(level, depth, wide):
        for side, row, rows, col, cols in (
            ((-1, 0), -depth, depth, -wide, I + 2 * wide),
            ((1, 0), J, depth, -wide, I + 2 * wide),
            ((0, -1), -depth, J + 2 * depth, -wide, wide),
            ((0, 1), -depth, J + 2 * depth, I, wide),
        ):
            @pl.when(jnp.logical_not(exists(side)))
            def _(row=row, rows=rows, col=col, cols=cols):
                view(level, row, rows, col, cols)[...] = jnp.zeros((rows, cols, M), jnp.float32)

    base = 0
    for depth in ROUNDS:
        clear(levels[base], depth, TILE)
        base += depth
    pl.semaphore_wait(barrier, near)

    def copy_of(number):
        name, (dj, di), depth = MESSAGES[number]
        src_row, dst_row, rows = {-1: (0, J, depth), 0: (0, 0, J), 1: (J - depth, -depth, depth)}[dj]
        src_col, dst_col, cols = {-1: (0, I, TILE), 0: (0, 0, I), 1: (I - TILE, -TILE, TILE)}[di]
        return pltpu.make_async_remote_copy(
            src_ref=view(arrays[name], src_row, rows, src_col, cols),
            dst_ref=view(arrays[name], dst_row, rows, dst_col, cols),
            send_sem=send_sem.at[number], recv_sem=recv_sem.at[number],
            device_id=peer((dj, di)), device_id_type=MESH)

    def start(*names):
        for number, (name, side, _) in enumerate(MESSAGES):
            if name in names:
                pl.when(exists(side))(lambda number=number: copy_of(number).start())

    def receive(*names):
        for number, (name, side, _) in enumerate(MESSAGES):
            if name in names:
                pl.when(exists((-side[0], -side[1])))(lambda number=number: copy_of(number).wait_recv())

    def update(k, row, rows, col, cols):
        value = advance(levels[k - 1], fj, fi, row, rows, col, cols)
        if k == STEPS:
            end[pl.ds(row, rows), pl.ds(col, cols), :] = value
        else:
            view(levels[k], row, rows, col, cols)[...] = value

    def sweep(k, first, last, col, cols, most):
        rows = chunk_of(last - first, most)

        def body(turn, _):
            update(k, first + turn * rows, rows, col, cols)
            return 0

        lax.fori_loop(0, (last - first) // rows, body, 0)

    loads[0].wait()
    start(0)
    loads[1].wait()
    loads[2].wait()
    start("fj", "fi")
    base, flows_in = 0, False
    for depth in ROUNDS:
        for t in range(1, depth + 1):
            sweep(base + t, t, J - t, t, I - 2 * t, 6)
        receive(base)
        if depth > 1 and not flows_in:
            receive("fj", "fi")
            flows_in = True
        for t in range(1, depth + 1):
            m = depth - t
            sweep(base + t, -m, t, -m, I + 2 * m, 4)
            sweep(base + t, J - t, J + m, -m, I + 2 * m, 4)
            sweep(base + t, t, J - t, -m, depth, 15)
            sweep(base + t, t, J - t, I - t, depth, 15)
            if m:
                clear(levels[base + t], m, m)
        base += depth
        start(base)

    total = end[0]
    for row in range(1, J):
        total = total + end[row]
    own[...] = total

    def total_copy(source, other):
        return pltpu.make_async_remote_copy(
            src_ref=own, dst_ref=totals.at[source], send_sem=total_send.at[other], recv_sem=total_recv.at[source],
            device_id={"south": other, "east": e}, device_id_type=MESH)

    def give(turn, _):
        total_copy(s, s + turn).start()
        return 0

    lax.fori_loop(1, souths - s, give, 0)

    for number, (_, side, _) in enumerate(MESSAGES):
        pl.when(exists(side))(lambda number=number: copy_of(number).wait_send())

    def take(source, state):
        total_copy(source, s).wait_recv()
        return state + totals[source]

    state = lax.fori_loop(0, s, take, jnp.zeros_like(own))
    scale = 1.0 / (J * souths)
    for row in range(J):
        state = state + end[row]
        running[row] = state * scale

    def sent(turn, _):
        total_copy(s, s + turn).wait_send()
        return 0

    lax.fori_loop(1, souths - s, sent, 0)


def write_out(running, end, running_out, end_out, sems):
    copies = [pltpu.make_async_copy(running, running_out, sems.at[0]), pltpu.make_async_copy(end, end_out, sems.at[1])]
    for copy in copies:
        copy.start()
    for copy in copies:
        copy.wait()


def per_device(souths, easts, tracer, flow_j, flow_i):
    J, I, M = tracer.shape
    out = jax.ShapeDtypeStruct((J, I, M), jnp.float32)
    padded = pltpu.VMEM((J + 2 * DEEP, I + 2 * TILE, M), jnp.float32)
    results = pl.pallas_call(
        functools.partial(kernel, souths, easts),
        out_shape=(out, out),
        in_specs=[pl.BlockSpec(memory_space=pl.ANY)] * 3,
        out_specs=(pl.BlockSpec(memory_space=pltpu.VMEM),) * 2,
        scratch_shapes=[padded] * 6
        + [
            pltpu.VMEM((I, M), jnp.float32),
            pltpu.VMEM((souths, I, M), jnp.float32),
            pltpu.SemaphoreType.DMA((3,)),
            pltpu.SemaphoreType.DMA((len(MESSAGES),)),
            pltpu.SemaphoreType.DMA((len(MESSAGES),)),
            pltpu.SemaphoreType.DMA((souths,)),
            pltpu.SemaphoreType.DMA((souths,)),
        ],
        compiler_params=pltpu.CompilerParams(collective_id=0, has_side_effects=True,
                                             vmem_limit_bytes=105 * 2 ** 19),
    )(tracer, flow_j, flow_i)
    return pl.pallas_call(
        write_out,
        out_shape=(out, out),
        in_specs=[pl.BlockSpec(memory_space=pltpu.VMEM)] * 2,
        out_specs=(pl.BlockSpec(memory_space=pl.ANY),) * 2,
        scratch_shapes=[pltpu.SemaphoreType.DMA((2,))],
        compiler_params=pltpu.CompilerParams(vmem_limit_bytes=2 ** 20),
    )(*results)


def solution(mesh):
    spec = P("south", "east", None)
    body = functools.partial(per_device, mesh.shape["south"], mesh.shape["east"])
    return jax.shard_map(body, mesh=mesh, in_specs=(spec,) * 3, out_specs=(spec,) * 2, check_vma=False)
```

time: 28.8 us -> 20 us (0.69)
  the two profiles are of different devices: /device:TPU:30 before, /device:TPU:24 now
where the time goes in v2:
time: 20 us; the launch traced here: 19.8 us
  Pallas kernels  19.2 us (96%)
  between operations  0.64 us (3%)
    pallas_call x1, Pallas kernels, per_device(): pl.pallas_call(functools.partial(kernel, souths, easts), out_shape=(out,...  18.2 us
    pallas_call x1, Pallas kernels, per_device(): pl.pallas_call(write_out, out_shape=(out, out), in_specs=[pl.BlockSpec(me...  0.99 us

profile of v2, /device:TPU:24, one launch (start us, length us, event | category | flops | bytes accessed | tf_op | source)
XLA Modules:
  0.0 19.8 jit_solution(17108406624038166851)
XLA Ops:
  0.6 18.2 %shard_map.50 = (f32[32,32,128]{2,1,0:T(8,128)S(1)}, f32[32,32,128]{2,1,0:T(8,128)S(1)}) custom-call(f32[32,32,128]{2,1,0:T(8,128)} %tracer.1, f32[32,32,128]{2,1,0:T(8,128)} %flow_j.1, f32[32,32,128]{2,1,0:T(8,128)} %flow_i.1), custom_call_target="tpu_custom_call" | custom-call | tf_op jit(solution)/shard_map/pallas_call | solution.py:212
  18.9 1.0 %shard_map.51 = (f32[32,32,128]{2,1,0:T(8,128)}, f32[32,32,128]{2,1,0:T(8,128)}) custom-call(f32[32,32,128]{2,1,0:T(8,128)S(1)} %get-tuple-element.4.running, f32[32,32,128]{2,1,0:T(8,128)S(1)} %get-tuple-element.5.end), custom_call_target="tpu_custom_call" | custom-call | tf_op jit(solution)/shard_map/pallas_call | solution.py:230

commit v3 on v2

--- a/solution.py
+++ b/solution.py
@@ -48,7 +48,7 @@
             - view(flow_i, *area)[...] * (upper_i - lower_i) + 0.05 * spread)
 
 
-def kernel(souths, easts, tracer, flow_j, flow_i, running, end, level0, level1, level2, level3, fj, fi, own, totals,
+def kernel(souths, easts, tracer, flow_j, flow_i, before, end, level0, level1, level2, level3, fj, fi, own, totals, ready,
            load_sem, send_sem, recv_sem, total_send, total_recv):
     J, I, M = tracer.shape
     s, e = lax.axis_index("south"), lax.axis_index("east")
@@ -68,21 +68,25 @@
         return {"south": s + side[0], "east": e + side[1]}
 
     barrier = pltpu.get_barrier_semaphore()
-    near = souths - 1
+    near = 0
     for side in SIDES:
-        if side[1] and (DEEP > 1 or not side[0]):
+        if 0 in side:
             near = near + exists(side).astype(jnp.int32)
 
             @pl.when(exists(side))
             def _(side=side):
                 pl.semaphore_signal(barrier, inc=1, device_id=peer(side), device_id_type=MESH)
 
-    def greet(turn, _):
-        other = lax.rem(s + turn, souths)
-        pl.semaphore_signal(barrier, inc=1, device_id={"south": other, "east": e}, device_id_type=MESH)
-        return 0
-
-    lax.fori_loop(1, souths, greet, 0)
+    stages = [2 ** k for k in range(1, souths.bit_length()) if 2 ** k < souths - 1]
+
+    def tell(stage, reach):
+        for ok, other in ((s >= reach, s - reach), (s + reach < souths, s + reach)):
+            @pl.when(ok)
+            def _(other=other):
+                pl.semaphore_signal(ready.at[stage], inc=1, device_id={"south": other, "east": e}, device_id_type=MESH)
+
+    def hear(stage, reach):
+        pl.semaphore_wait(ready.at[stage], (s >= reach).astype(jnp.int32) + (s + reach < souths).astype(jnp.int32))
 
     def clear(level, depth, wide):
         for side, row, rows, col, cols in (
@@ -104,16 +108,16 @@
     def copy_of(number):
         name, (dj, di), depth = MESSAGES[number]
         src_row, dst_row, rows = {-1: (0, J, depth), 0: (0, 0, J), 1: (J - depth, -depth, depth)}[dj]
-        src_col, dst_col, cols = {-1: (0, I, TILE), 0: (0, 0, I), 1: (I - TILE, -TILE, TILE)}[di]
+        src_col, dst_col, cols = {-1: (0, I, depth), 0: (0, 0, I), 1: (I - depth, -depth, depth)}[di]
         return pltpu.make_async_remote_copy(
             src_ref=view(arrays[name], src_row, rows, src_col, cols),
             dst_ref=view(arrays[name], dst_row, rows, dst_col, cols),
             send_sem=send_sem.at[number], recv_sem=recv_sem.at[number],
             device_id=peer((dj, di)), device_id_type=MESH)
 
-    def start(*names):
+    def start(*names, corners=False):
         for number, (name, side, _) in enumerate(MESSAGES):
-            if name in names:
+            if name in names and all(side) == corners:
                 pl.when(exists(side))(lambda number=number: copy_of(number).start())
 
     def receive(*names):
@@ -142,14 +146,23 @@
     loads[1].wait()
     loads[2].wait()
     start("fj", "fi")
-    base, flows_in = 0, False
-    for depth in ROUNDS:
+    base = 0
+    for turn, depth in enumerate(ROUNDS):
         for t in range(1, depth + 1):
             sweep(base + t, t, J - t, t, I - 2 * t, 6)
+        if turn == 1 and stages:
+            hear(0, stages[0])
+            for stage, reach in enumerate(stages[1:], 1):
+                tell(stage, reach)
+                if stage < len(stages) - 1:
+                    hear(stage, reach)
         receive(base)
-        if depth > 1 and not flows_in:
+        if turn == 0:
+            start("fj", "fi", corners=True)
+            if stages:
+                tell(0, stages[0])
+        if turn == 1:
             receive("fj", "fi")
-            flows_in = True
         for t in range(1, depth + 1):
             m = depth - t
             sweep(base + t, -m, t, -m, I + 2 * m, 4)
@@ -160,6 +173,9 @@
                 clear(levels[base + t], m, m)
         base += depth
         start(base)
+        start(base, corners=True)
+    if len(stages) > 1:
+        hear(len(stages) - 1, stages[-1])
 
     total = end[0]
     for row in range(1, J):
@@ -184,11 +200,7 @@
         total_copy(source, s).wait_recv()
         return state + totals[source]
 
-    state = lax.fori_loop(0, s, take, jnp.zeros_like(own))
-    scale = 1.0 / (J * souths)
-    for row in range(J):
-        state = state + end[row]
-        running[row] = state * scale
+    before[...] = lax.fori_loop(0, s, take, jnp.zeros_like(own))
 
     def sent(turn, _):
         total_copy(s, s + turn).wait_send()
@@ -197,10 +209,19 @@
     lax.fori_loop(1, souths - s, sent, 0)
 
 
-def write_out(running, end, running_out, end_out, sems):
-    copies = [pltpu.make_async_copy(running, running_out, sems.at[0]), pltpu.make_async_copy(end, end_out, sems.at[1])]
-    for copy in copies:
-        copy.start()
+def write_out(scale, before, end, running_out, end_out, running, sems):
+    J = end.shape[0]
+    rows = chunk_of(J, 8)
+    copies = [pltpu.make_async_copy(end, end_out, sems.at[0])]
+    copies[0].start()
+    state = before[...]
+    for chunk in range(J // rows):
+        for row in range(chunk * rows, (chunk + 1) * rows):
+            state = state + end[row]
+            running[row] = state * scale
+        part = pl.ds(chunk * rows, rows)
+        copies.append(pltpu.make_async_copy(running.at[part], running_out.at[part], sems.at[1 + chunk]))
+        copies[-1].start()
     for copy in copies:
         copy.wait()
 
@@ -211,13 +232,14 @@
     padded = pltpu.VMEM((J + 2 * DEEP, I + 2 * TILE, M), jnp.float32)
     results = pl.pallas_call(
         functools.partial(kernel, souths, easts),
-        out_shape=(out, out),
+        out_shape=(jax.ShapeDtypeStruct((I, M), jnp.float32), out),
         in_specs=[pl.BlockSpec(memory_space=pl.ANY)] * 3,
         out_specs=(pl.BlockSpec(memory_space=pltpu.VMEM),) * 2,
         scratch_shapes=[padded] * 6
         + [
             pltpu.VMEM((I, M), jnp.float32),
             pltpu.VMEM((souths, I, M), jnp.float32),
+            pltpu.SemaphoreType.REGULAR((souths.bit_length(),)),
             pltpu.SemaphoreType.DMA((3,)),
             pltpu.SemaphoreType.DMA((len(MESSAGES),)),
             pltpu.SemaphoreType.DMA((len(MESSAGES),)),
@@ -225,15 +247,15 @@
             pltpu.SemaphoreType.DMA((souths,)),
         ],
         compiler_params=pltpu.CompilerParams(collective_id=0, has_side_effects=True,
-                                             vmem_limit_bytes=105 * 2 ** 19),
+                                             vmem_limit_bytes=106 * 2 ** 19),
     )(tracer, flow_j, flow_i)
     return pl.pallas_call(
-        write_out,
+        functools.partial(write_out, 1.0 / (J * souths)),
         out_shape=(out, out),
         in_specs=[pl.BlockSpec(memory_space=pltpu.VMEM)] * 2,
         out_specs=(pl.BlockSpec(memory_space=pl.ANY),) * 2,
-        scratch_shapes=[pltpu.SemaphoreType.DMA((2,))],
-        compiler_params=pltpu.CompilerParams(vmem_limit_bytes=2 ** 20),
+        scratch_shapes=[pltpu.VMEM((J, I, M), jnp.float32), pltpu.SemaphoreType.DMA((J + 1,))],
+        compiler_params=pltpu.CompilerParams(vmem_limit_bytes=2 ** 21),
     )(*results)
 
 

time: 20 us -> 18.4 us (0.920)
  Pallas kernels: 19.2 us -> 17.7 us
    pallas_call x2, Pallas kernels: 19.2 us -> 17.7 us  [the longest x1 16.4 us: per_device(): pl.pallas_call(functools.partial(kernel, souths, easts), out_shape=(jax.S...]
where the time goes in v3:
time: 18.4 us; the launch traced here: 18.3 us
  Pallas kernels  17.7 us (96%)
  between operations  0.64 us (3%)
    pallas_call x1, Pallas kernels, per_device(): pl.pallas_call(functools.partial(kernel, souths, easts), out_shape=(jax.S...  16.4 us
    pallas_call x1, Pallas kernels, per_device(): pl.pallas_call(functools.partial(write_out, 1.0 / (J * souths)), out_shap...  1.25 us

profile of v3, /device:TPU:24, one launch (start us, length us, event | category | flops | bytes accessed | tf_op | source)
XLA Modules:
  0.0 18.3 jit_solution(17956424618189632838)
XLA Ops:
  0.6 16.4 %shard_map.50 = (f32[32,128]{1,0:T(8,128)S(1)}, f32[32,32,128]{2,1,0:T(8,128)S(1)}) custom-call(f32[32,32,128]{2,1,0:T(8,128)} %tracer.1, f32[32,32,128]{2,1,0:T(8,128)} %flow_j.1, f32[32,32,128]{2,1,0:T(8,128)} %flow_i.1), custom_call_target="tpu_custom_call" | custom-call | tf_op jit(solution)/shard_map/pallas_call | solution.py:233
  17.0 1.3 %shard_map.51 = (f32[32,32,128]{2,1,0:T(8,128)}, f32[32,32,128]{2,1,0:T(8,128)}) custom-call(f32[32,128]{1,0:T(8,128)S(1)} %get-tuple-element.4.before, f32[32,32,128]{2,1,0:T(8,128)S(1)} %get-tuple-element.5.end), custom_call_target="tpu_custom_call" | custom-call | tf_op jit(solution)/shard_map/pallas_call | solution.py:252
